TPU v7x, 256 devices: a whole 4x4x8 slice. The times are simulated.
256 devices in a mesh: dp: 8 (over y, core), expert: 8 (over z), tile: 4 (over x).
Axes of the slice: x: 4, y: 4, z: 8, core: 2. Of those that a mesh axis runs over, the one named last changes fastest.
Arguments:
- tokens: bfloat16 [4096, 4096], P(('dp', 'expert'), 'tile'), may hold values from -6 to 6
- hidden: bfloat16 [4096, 2, 7168], P(('dp', 'expert'), None, 'tile'), may hold values from -6 to 6
- routes: int32 [4096, 2], P(('dp', 'expert')), may hold values from 0 to 7, all different within a row; in each aligned block of 64 rows (0 to 63, 64 to 127, ...) at most 24 rows name the same one
- lengths: int32 [64], P(('dp', 'expert')), may hold values from 1 to 64, as said below
Outputs:
- hessian_in: float32 [8, 4096, 4096], P('expert', 'tile', 'dp')
- hessian_down: float32 [8, 7168, 7168], P('expert', 'tile', 'dp')
Inputs may be any that keep to these rules, and one draw needn't show every extreme that they name: `routes`: in each aligned block of 64 rows (the rows of one group) no expert is named by more than 24 rows, a bound that some block reaches. The live rows of group g are its first lengths[g] rows; the last group is full.
All inputs are finite; a program needn't handle non-finite values.
Results may differ from a plain program's by a relative error of at most 0.0003.
Values may be sent and summed in bfloat16 or wider, within the bound.
A program may use at most 64 MiB of HBM per device.

v0:
```python
import jax
import jax.numpy as jnp
from jax import lax
from jax.sharding import PartitionSpec as P


def sent_together(arrays, axis, split_dim, concat_dim, along):
    widths = [a.shape[along] for a in arrays]
    both = jnp.concatenate(arrays, axis=along)
    out = lax.all_to_all(both, axis, split_axis=split_dim, concat_axis=concat_dim, tiled=True)
    return tuple(jnp.split(out, [sum(widths[:k]) for k in range(1, len(widths))], axis=along))


def from_everyone(value, axis):
    copies = jnp.broadcast_to(value, (lax.axis_size(axis), *value.shape))
    return lax.all_to_all(copies, axis, split_axis=0, concat_axis=0, tiled=True)


def of_everyone(value, axis):
    everything = from_everyone(value, axis)
    return jnp.sum(everything, axis=0)


def side_by_side(arrays, axis, dim, along):
    ends, at = ([], 0)
    for a in arrays[:-1]:
        at += a.shape[along]
        ends.append(at)
    both = jnp.concatenate(arrays, axis=along)
    return tuple(jnp.split(lax.all_gather(both, axis, axis=dim, tiled=True), ends, axis=along))


def contract(left, right):
    return lax.dot_general(
        left, right, (((0,), (0,)), ((), ())), preferred_element_type=jnp.float32
    )


def dispatch_tables(routes, live_count, experts, share_size, senders):
    token_count = routes.shape[0]
    top_count = routes.shape[1]
    flat_routes = routes.reshape(token_count * top_count)
    pair_index = jnp.arange(token_count * top_count, dtype=jnp.int32)
    pair_live = pair_index // top_count < live_count
    expert_ids = jnp.arange(experts, dtype=jnp.int32)
    onehot = ((flat_routes[:, None] == expert_ids[None, :]) & pair_live[:, None]).astype(
        jnp.float32
    )
    before = jnp.cumsum(onehot, axis=0) - onehot
    position = jnp.sum(before * onehot, axis=1).astype(jnp.int32)
    target = (
        position // share_size * (experts * share_size)
        + flat_routes * share_size
        + position % share_size
    )
    slot_total = senders * experts * share_size
    placed = (target[None, :] == jnp.arange(slot_total, dtype=jnp.int32)[:, None]) & pair_live[
        None, :
    ]
    return (placed.astype(jnp.float32), jnp.sum(onehot, axis=0))


def on_device(tokens, hidden, routes, lengths):
    experts = lax.axis_size("expert")
    senders = lax.axis_size("dp")
    token_count = tokens.shape[0]
    top_count = routes.shape[1]
    share_size = (5 * token_count + 2 * experts * senders - 1) // (2 * experts * senders)
    placed, local_counts = dispatch_tables(routes, lengths[0], experts, share_size, senders)
    slot_total = placed.shape[0]
    by_token = jnp.sum(placed.reshape(slot_total, token_count, top_count), axis=2).astype(
        jnp.bfloat16
    )
    send_tokens = jnp.dot(by_token, tokens, preferred_element_type=jnp.float32).astype(jnp.bfloat16)
    flat_hidden = hidden.reshape(token_count * top_count, hidden.shape[2])
    send_hidden = jnp.dot(
        placed.astype(jnp.bfloat16), flat_hidden, preferred_element_type=jnp.float32
    ).astype(jnp.bfloat16)
    slot_tokens, slot_hidden = sent_together((send_tokens, send_hidden), ("dp", "expert"), 0, 0, 1)
    global_counts = of_everyone(local_counts, ("dp", "expert"))
    own_expert = lax.axis_index("expert")
    own_count = jnp.sum(
        jnp.where(jnp.arange(experts, dtype=jnp.int32) == own_expert, global_counts, 0.0)
    )
    factor = 2.0 / jnp.maximum(own_count, 1.0)
    full_tokens, full_hidden = (
        lax.all_gather(slot_tokens, "tile", axis=1, tiled=True),
        lax.all_gather(slot_hidden, "tile", axis=1, tiled=True),
    )
    column_tokens, column_hidden = (
        lax.all_to_all(full_tokens, "dp", split_axis=1, concat_axis=0, tiled=True),
        lax.all_to_all(full_hidden, "dp", split_axis=1, concat_axis=0, tiled=True),
    )
    pieces = side_by_side((slot_tokens, slot_hidden), "dp", 0, 1)
    gram_tokens = contract(pieces[0], column_tokens)
    gram_hidden = contract(pieces[1], column_hidden)
    return ((gram_tokens * factor)[None], (gram_hidden * factor)[None])


def solution(mesh):
    placed = (
        P(("dp", "expert"), "tile"),
        P(("dp", "expert"), None, "tile"),
        P(("dp", "expert"), None),
        P(("dp", "expert")),
    )
    return jax.shard_map(
        on_device,
        mesh=mesh,
        in_specs=placed,
        out_specs=(P("expert", "tile", "dp"), P("expert", "tile", "dp")),
        check_vma=False,
    )
```

profile of v0, /device:TPU:1, one launch (start us, length us, event | category | flops | bytes accessed | tf_op | source)
XLA Modules:
  0.0 226.2 jit_solution(10405702550066354825)
XLA Ops:
  7.2 0.0 copy-start
  7.2 0.0 all-gather.8.cloned.1.call-start
  7.9 0.8 copy.33
  8.7 0.1 eq.43
  8.8 0.1 fusion.11
  8.9 0.2 reduce_window_sum.11
  9.1 0.2 fusion.12
  9.3 0.1 rem.32
  9.5 0.1 copy.34
  9.5 0.1 div.25
  9.7 0.1 copy.36
  9.8 0.2 ne.82
  9.9 0.1 copy.35
  10.1 1.2 reshape.98
  11.2 0.7 fusion.18
  11.9 0.1 convert_reduce_fusion
  12.1 0.0 copy-done
  12.1 0.3 convolution_convert_fusion.1
  12.3 0.3 convolution_convert_fusion
  12.7 0.1 pad_maximum_fusion
  12.8 0.5 all_to_all.40
  13.3 49.6 %all_to_all.56 = bf16[64,3,2816]{2,1,0:T(4,128)(2,1)S(1)} all-to-all(bf16[64,3,2816]{2,1,0:T(4,128)(2,1)S(1)} %all_to_all.40), channel_id=1, replica_groups=mesh['dp'=8,'expert'=8,'tile'=4] {'dp','expert'}, dimensions={0} | all-to-all | bytes 2162688 | tf_op jit(solution)/shard_map/all_to_all | solution.py:10
  62.8 0.9 all_to_all.42
  63.8 0.0 copy-start.1
  63.8 1.0 split.19
  64.8 0.0 all-gather.8.cloned.1.call-update
  64.8 0.0 all-gather.6.cloned.1.call-start
  64.8 0.8 split.17
  65.7 0.0 all-gather.6.cloned.1.call-update
  65.7 0.0 all-gather.4.cloned.1.call-start
  65.7 0.0 copy-done.1
  65.7 0.7 all-gather.4.cloned.1.call-update
  66.4 0.6 broadcast_in_dim.18
  67.0 6.7 %all-to-all-start.2 = ((f32[64,1,8]{2,1,0:T(1,128)}), f32[64,1,8]{2,1,0:T(1,128)S(1)}, u32[]{:S(2)}, u32[]{:S(2)}) async-start(f32[64,1,8]{2,1,0:T(1,128)} %broadcast_in_dim.18), calls=%async_computation.2 | async-start | bytes 65536 | tf_op jit(solution)/shard_map/all_to_all | solution.py:16
  73.8 27.1 %all-gather.8.cloned.1.call-done = bf16[192,7168]{1,0:T(8,128)(2,1)} async-done(((bf16[192,1792]{1,0:T(8,128)(2,1)}), bf16[192,7168]{1,0:T(8,128)(2,1)}) %all-gather.8.cloned.1.call-update) | async-done | bytes 2752528 | tf_op jit(solution)/shard_map/all_gather | solution.py:88
  100.9 3.7 %copy.49 = bf16[24,8,8,896]{3,2,0,1:T(8,128)(2,1)} copy(bf16[24,8,8,896]{3,2,1,0:T(8,128)(2,1)} %bitcast.27) | data formatting | bytes 5505024 | tf_op jit(solution)/shard_map/all_to_all | solution.py:92
  104.6 0.0 all-to-all-done.2
  104.6 5.1 %all-to-all-start.3 = ((bf16[192,8,896]{2,0,1:T(8,128)(2,1)}), bf16[192,8,896]{2,0,1:T(8,128)(2,1)S(1)}, u32[]{:S(2)}, u32[]{:S(2)}) async-start(bf16[192,8,896]{2,0,1:T(8,128)(2,1)} %bitcast.22), calls=%async_computation.3 | async-start | bytes 5505024 | tf_op jit(solution)/shard_map/all_to_all | solution.py:92
  109.7 22.2 %all-gather.6.cloned.1.call-done = bf16[192,4096]{1,0:T(8,128)(2,1)} async-done(((bf16[192,1024]{1,0:T(8,128)(2,1)}), bf16[192,4096]{1,0:T(8,128)(2,1)}) %all-gather.6.cloned.1.call-update) | async-done | bytes 1572880 | tf_op jit(solution)/shard_map/all_gather | solution.py:87
  131.9 2.7 %copy.50 = bf16[24,8,8,512]{3,2,0,1:T(8,128)(2,1)} copy(bf16[24,8,8,512]{3,2,1,0:T(8,128)(2,1)} %bitcast.28) | data formatting | bytes 3145728 | tf_op jit(solution)/shard_map/all_to_all | solution.py:91
  134.6 8.4 %all-to-all-done.3 = bf16[192,8,896]{2,0,1:T(8,128)(2,1)S(1)} async-done(((bf16[192,8,896]{2,0,1:T(8,128)(2,1)}), bf16[192,8,896]{2,0,1:T(8,128)(2,1)S(1)}, u32[]{:S(2)}, u32[]{:S(2)}) %all-to-all-start.3) | async-done | bytes 2752544 | tf_op jit(solution)/shard_map/all_to_all | solution.py:92
  142.9 5.2 %all-to-all-start.1 = ((bf16[192,8,512]{2,0,1:T(8,128)(2,1)}), bf16[192,8,512]{2,0,1:T(8,128)(2,1)}, u32[]{:S(2)}, u32[]{:S(2)}) async-start(bf16[192,8,512]{2,0,1:T(8,128)(2,1)} %bitcast.23), calls=%async_computation.1 | async-start | bytes 3145728 | tf_op jit(solution)/shard_map/all_to_all | solution.py:91
  148.1 0.1 reduce_sum.48
  148.2 0.6 fusion.22
  149.5 55.0 %all-gather.4.cloned.1.call-done = bf16[1536,2816]{1,0:T(8,128)(2,1)} async-done(((bf16[192,2816]{1,0:T(8,128)(2,1)}), bf16[1536,2816]{1,0:T(8,128)(2,1)}) %all-gather.4.cloned.1.call-update) | async-done | bytes 8650768 | tf_op jit(solution)/shard_map/all_gather | solution.py:30
  204.5 9.6 %multiply_bitcast_fusion = f32[1,1792,896]{2,1,0:T(8,128)} fusion(bf16[1536,896]{1,0:T(8,128)(2,1)S(1)} %bitcast.26, bf16[1536,2816]{1,0:T(8,128)(2,1)} %all-gather.4.cloned.1.call-done, f32[]{:T(128)S(6)} %div.27), kind=kOutput, calls=%fused_computation | convolution fusion | flops 4934107136 | bytes 14680068 | tf_op jit(solution)/shard_map/dot_general | solution.py:34
  214.2 0.0 all-to-all-done.1
  214.2 5.5 %multiply_bitcast_fusion.1 = f32[1,1024,512]{2,1,0:T(8,128)} fusion(bf16[1536,512]{1,0:T(8,128)(2,1)} %bitcast.2, bf16[1536,2816]{1,0:T(8,128)(2,1)} %all-gather.4.cloned.1.call-done, f32[]{:T(128)S(6)} %div.27), kind=kOutput, calls=%fused_computation.7 | convolution fusion | flops 1611137024 | bytes 6815748 | tf_op jit(solution)/shard_map/dot_general | solution.py:34
  (4 shorter events, 0.1 us)
Async XLA Ops:
  7.2 4.9 %copy-start = (bf16[64,1024]{1,0:T(8,128)(2,1)S(1)}, bf16[64,1024]{1,0:T(8,128)(2,1)}, u32[]{:S(2)}) copy-start(bf16[64,1024]{1,0:T(8,128)(2,1)} %param.4) | copy-start | bytes 393220
  7.2 93.7 %all-gather.8.cloned.1.call-start = ((), (), s32[]{:S(2)}) async-start(), calls=%async_computation.6 | async-start | bytes 3440640 | tf_op jit(solution)/shard_map/all_gather | solution.py:88
  63.8 2.0 copy-start.1
  64.8 67.1 %all-gather.6.cloned.1.call-start = ((), (), s32[]{:S(2)}) async-start(), calls=%async_computation.5 | async-start | bytes 1966080 | tf_op jit(solution)/shard_map/all_gather | solution.py:87
  65.7 138.8 %all-gather.4.cloned.1.call-start = ((), (), s32[]{:S(2)}) async-start(), calls=%async_computation.4 | async-start | bytes 9732096 | tf_op jit(solution)/shard_map/all_gather | solution.py:30
  67.0 37.5 %all-to-all-start.2 = ((f32[64,1,8]{2,1,0:T(1,128)}), f32[64,1,8]{2,1,0:T(1,128)S(1)}, u32[]{:S(2)}, u32[]{:S(2)}) async-start(f32[64,1,8]{2,1,0:T(1,128)} %broadcast_in_dim.18), calls=%async_computation.2 | async-start | bytes 65536 | tf_op jit(solution)/shard_map/all_to_all | solution.py:16
  104.6 38.4 %all-to-all-start.3 = ((bf16[192,8,896]{2,0,1:T(8,128)(2,1)}), bf16[192,8,896]{2,0,1:T(8,128)(2,1)S(1)}, u32[]{:S(2)}, u32[]{:S(2)}) async-start(bf16[192,8,896]{2,0,1:T(8,128)(2,1)} %bitcast.22), calls=%async_computation.3 | async-start | bytes 5505024 | tf_op jit(solution)/shard_map/all_to_all | solution.py:92
  142.9 71.2 %all-to-all-start.1 = ((bf16[192,8,512]{2,0,1:T(8,128)(2,1)}), bf16[192,8,512]{2,0,1:T(8,128)(2,1)}, u32[]{:S(2)}, u32[]{:S(2)}) async-start(bf16[192,8,512]{2,0,1:T(8,128)(2,1)} %bitcast.23), calls=%async_computation.1 | async-start | bytes 3145728 | tf_op jit(solution)/shard_map/all_to_all | solution.py:91
Sparse Core Ops, SparseCore 0:
  64.9 35.9 all-gather.7
  102.7 29.1 all-gather.5
  133.7 70.7 all-gather.3
where the time goes:
time: 227 us; the launch traced here: 226 us
  waiting for transfers between devices  113 us (50%)
  blocking collectives  49.6 us (22%)
  starting transfers between devices  17.1 us (8%)
  matrix products  15.8 us (7%)
  between operations  15.3 us (7%)
  local copies, waits for them, and re-layouts  13 us (6%)
    all_gather x1, waiting for transfers between devices, side_by_side(): lax.all_gather(both, axis, axis=dim, tiled=True)  55 us
    all_to_all x1, blocking collectives, sent_together(): lax.all_to_all(both, axis, split_axis=split_dim, concat_axis=concat_dim,...  49.6 us
    all_gather x1, waiting for transfers between devices, on_device(): lax.all_gather(slot_hidden, 'tile', axis=1, tiled=True)  27.1 us
    all_gather x1, waiting for transfers between devices, on_device(): lax.all_gather(slot_tokens, 'tile', axis=1, tiled=True)  22.2 us
    dot_general x2, matrix products, contract(): lax.dot_general(left, right, (((0,), (0,)), ((), ())), preferred_element_...  15.2 us
    all_to_all x1, waiting for transfers between devices, on_device(): lax.all_to_all(full_hidden, 'dp', split_axis=1, concat_axis=0, tiled=True)  8.35 us
    all_to_all x1, starting transfers between devices, from_everyone(): return lax.all_to_all(copies, axis, split_axis=0, concat_axis=0, tiled=True)  6.72 us
    all_to_all x1, starting transfers between devices, on_device(): lax.all_to_all(full_tokens, 'dp', split_axis=1, concat_axis=0, tiled=True)  5.17 us
  transfers between devices with their start and end apart: 6, of which 4 were waited for; matrix products, arithmetic and copies ran while one was open for 8% of the time, Pallas kernels for 0%

commit v1 on v0

--- a/solution.py
+++ b/solution.py
@@ -85,7 +85,9 @@
     factor = 2.0 / jnp.maximum(own_count, 1.0)
     full_tokens, full_hidden = (
         lax.all_gather(slot_tokens, "tile", axis=1, tiled=True),
-        lax.all_gather(slot_hidden, "tile", axis=1, tiled=True),
+        jnp.concatenate(
+            lax.all_to_all(jnp.stack([slot_hidden] * lax.axis_size("tile")), "tile", 0, 0), axis=1
+        ),
     )
     column_tokens, column_hidden = (
         lax.all_to_all(full_tokens, "dp", split_axis=1, concat_axis=0, tiled=True),

time: 227 us -> 234 us (1.031)
  waiting for transfers between devices: 113 us -> 63.8 us
  blocking collectives: 49.6 us -> 98.4 us
  local copies, waits for them, and re-layouts: 13 us -> 20.1 us
    all_gather x1, waiting for transfers between devices: 55 us -> 0.02 us  [side_by_side(): lax.all_gather(both, axis, axis=dim, tiled=True)]
    all_to_all x0 -> x1, blocking collectives: none -> 48.9 us  [on_device(): lax.all_to_all(jnp.stack([slot_hidden] * lax.axis_size('tile')), 'tile',...]
    all_to_all x1, waiting for transfers between devices: 8.35 us -> 53.5 us  [on_device(): lax.all_to_all(full_hidden, 'dp', split_axis=1, concat_axis=0, tiled=True)]
    all_gather x1 -> x0, waiting for transfers between devices: 27.1 us -> none  [on_device(): lax.all_gather(slot_hidden, 'tile', axis=1, tiled=True)]
    all_gather x1, waiting for transfers between devices: 22.2 us -> 0.01 us  [on_device(): lax.all_gather(slot_tokens, 'tile', axis=1, tiled=True)]
    all_to_all x1, waiting for transfers between devices: 0.01 us -> 9.72 us  [on_device(): lax.all_to_all(full_tokens, 'dp', split_axis=1, concat_axis=0, tiled=True)]
    reshape x0 -> x1, local copies, waits for them, and re-layouts: none -> 3.66 us  [on_device(): jnp.concatenate(lax.all_to_all(jnp.stack([slot_hidden] * lax.axis_size('t...]
    all_to_all x1 -> x2, local copies, waits for them, and re-layouts: 3.69 us -> 6.57 us  [on_device(): lax.all_to_all(full_hidden, 'dp', split_axis=1, concat_axis=0, tiled=True)]
  transfers between devices with their start and end apart: 6 -> 5, of which waited for: 4 -> 2; matrix products, arithmetic and copies ran while one was open for 8% -> 9% of each run, Pallas kernels for 0% -> 0%
where the time goes in v1:
time: 234 us; the launch traced here: 233 us
  blocking collectives  98.4 us (42%)
  waiting for transfers between devices  63.8 us (27%)
  local copies, waits for them, and re-layouts  20.1 us (9%)
  starting transfers between devices  17.6 us (8%)
  matrix products  15.7 us (7%)
  between operations  15.6 us (7%)
    all_to_all x1, waiting for transfers between devices, on_device(): lax.all_to_all(full_hidden, 'dp', split_axis=1, concat_axis=0, tiled=True)  53.5 us
    all_to_all x1, blocking collectives, sent_together(): lax.all_to_all(both, axis, split_axis=split_dim, concat_axis=concat_dim,...  49.6 us
    all_to_all x1, blocking collectives, on_device(): lax.all_to_all(jnp.stack([slot_hidden] * lax.axis_size('tile')), 'tile',...  48.9 us
    dot_general x2, matrix products, contract(): lax.dot_general(left, right, (((0,), (0,)), ((), ())), preferred_element_...  15.1 us
    all_to_all x1, waiting for transfers between devices, on_device(): lax.all_to_all(full_tokens, 'dp', split_axis=1, concat_axis=0, tiled=True)  9.72 us
    all_to_all x1, starting transfers between devices, from_everyone(): return lax.all_to_all(copies, axis, split_axis=0, concat_axis=0, tiled=True)  7.91 us
    all_to_all x2, local copies, waits for them, and re-layouts, on_device(): lax.all_to_all(full_hidden, 'dp', split_axis=1, concat_axis=0, tiled=True)  6.57 us
    all_to_all x1, starting transfers between devices, on_device(): lax.all_to_all(full_hidden, 'dp', split_axis=1, concat_axis=0, tiled=True)  4.9 us
  transfers between devices with their start and end apart: 5, of which 2 were waited for; matrix products, arithmetic and copies ran while one was open for 9% of the time, Pallas kernels for 0%

profile of v1, /device:TPU:1, one launch (start us, length us, event | category | flops | bytes accessed | tf_op | source)
XLA Modules:
  0.0 233.3 jit_solution(17416433230416607905)
XLA Ops:
  7.2 0.0 copy-start
  7.2 0.0 all-gather.5.cloned.1.call-start
  7.9 0.8 copy.42
  8.7 0.1 eq.43
  8.8 0.1 fusion.11
  8.9 0.2 reduce_window_sum.11
  9.1 0.2 fusion.12
  9.3 0.1 rem.32
  9.5 0.1 copy.43
  9.5 0.1 div.25
  9.7 0.1 copy.45
  9.8 0.2 ne.82
  9.9 0.1 copy.44
  10.1 1.2 reshape.105
  11.2 0.7 fusion.18
  11.9 0.1 convert_reduce_fusion
  12.1 0.0 copy-done
  12.1 0.3 convolution_convert_fusion.1
  12.4 0.3 convolution_convert_fusion
  12.7 0.1 pad_maximum_fusion
  12.8 0.5 all_to_all.43
  13.3 49.6 %all_to_all.61 = bf16[64,3,2816]{2,1,0:T(4,128)(2,1)S(1)} all-to-all(bf16[64,3,2816]{2,1,0:T(4,128)(2,1)S(1)} %all_to_all.43), channel_id=1, replica_groups=mesh['dp'=8,'expert'=8,'tile'=4] {'dp','expert'}, dimensions={0} | all-to-all | bytes 2162688 | tf_op jit(solution)/shard_map/all_to_all | solution.py:10
  62.8 0.9 all_to_all.45
  63.8 0.0 copy-start.1
  63.8 0.9 split.17
  64.6 0.0 all-gather.5.cloned.1.call-update
  64.7 0.0 all-gather.3.cloned.1.call-start
  64.7 0.2 copy-done.1
  64.9 0.5 all-gather.3.cloned.1.call-update
  65.4 1.1 split.19
  66.6 0.2 stack.2
  66.7 48.9 %all_to_all.62 = bf16[4,192,1792]{2,1,0:T(8,128)(2,1)S(1)} all-to-all(bf16[4,192,1792]{2,1,0:T(8,128)(2,1)S(1)} %stack.2), channel_id=1, replica_groups=mesh['dp'=8,'expert'=8,'tile'=4] {'tile'}, dimensions={0} | all-to-all | bytes 5505024 | tf_op jit(solution)/shard_map/all_to_all | solution.py:89
  115.6 0.6 broadcast_in_dim.18
  116.2 7.9 %all-to-all-start.2 = ((f32[64,1,8]{2,1,0:T(1,128)}), f32[64,1,8]{2,1,0:T(1,128)S(1)}, u32[]{:S(2)}, u32[]{:S(2)}) async-start(f32[64,1,8]{2,1,0:T(1,128)} %broadcast_in_dim.18), calls=%async_computation.2 | async-start | bytes 65536 | tf_op jit(solution)/shard_map/all_to_all | solution.py:16
  124.2 3.7 %copy.52 = bf16[192,4,1792]{2,1,0:T(4,128)(2,1)} copy(bf16[192,4,1792]{2,0,1:T(8,128)(2,1)S(1)} %bitcast.23) | data formatting | bytes 5505024 | tf_op jit(solution)/shard_map/reshape | solution.py:88
  127.8 4.6 %all_to_all.52 = bf16[192,8,896]{2,1,0:T(8,128)(2,1)S(1)} reshape(bf16[192,4,1792]{2,1,0:T(4,128)(2,1)} %copy.52) | data formatting | bytes 5505024 | tf_op jit(solution)/shard_map/all_to_all | solution.py:94
  132.4 2.0 copy.53
  134.4 0.0 all-to-all-done.2
  134.4 4.9 %all-to-all-start.4 = ((bf16[192,8,896]{2,0,1:T(8,128)(2,1)}), bf16[192,8,896]{2,0,1:T(8,128)(2,1)S(1)}, u32[]{:S(2)}, u32[]{:S(2)}) async-start(bf16[192,8,896]{2,0,1:T(8,128)(2,1)} %copy.53), calls=%async_computation.4 | async-start | bytes 5505024 | tf_op jit(solution)/shard_map/all_to_all | solution.py:94
  139.3 2.7 %copy.57 = bf16[24,8,8,512]{3,2,0,1:T(8,128)(2,1)} copy(bf16[24,8,8,512]{3,2,1,0:T(8,128)(2,1)} %bitcast.25) | data formatting | bytes 3145728 | tf_op jit(solution)/shard_map/all_to_all | solution.py:93
  142.0 53.5 %all-to-all-done.4 = bf16[192,8,896]{2,0,1:T(8,128)(2,1)S(1)} async-done(((bf16[192,8,896]{2,0,1:T(8,128)(2,1)}), bf16[192,8,896]{2,0,1:T(8,128)(2,1)S(1)}, u32[]{:S(2)}, u32[]{:S(2)}) %all-to-all-start.4) | async-done | bytes 2752544 | tf_op jit(solution)/shard_map/all_to_all | solution.py:94
  195.5 4.7 %all-to-all-start.1 = ((bf16[192,8,512]{2,0,1:T(8,128)(2,1)}), bf16[192,8,512]{2,0,1:T(8,128)(2,1)}, u32[]{:S(2)}, u32[]{:S(2)}) async-start(bf16[192,8,512]{2,0,1:T(8,128)(2,1)} %bitcast.20), calls=%async_computation.1 | async-start | bytes 3145728 | tf_op jit(solution)/shard_map/all_to_all | solution.py:93
  200.2 0.1 reduce_sum.48
  200.3 0.6 fusion.22
  201.6 0.0 all-gather.3.cloned.1.call-done
  201.6 9.6 %multiply_bitcast_fusion = f32[1,1792,896]{2,1,0:T(8,128)} fusion(bf16[1536,896]{1,0:T(8,128)(2,1)S(1)} %bitcast.24, bf16[1536,2816]{1,0:T(8,128)(2,1)} %all-gather.3.cloned.1.call-done, f32[]{:T(128)S(6)} %div.27), kind=kOutput, calls=%fused_computation | convolution fusion | flops 4934107136 | bytes 14680068 | tf_op jit(solution)/shard_map/dot_general | solution.py:34
  211.2 9.7 %all-to-all-done.1 = bf16[192,8,512]{2,0,1:T(8,128)(2,1)} async-done(((bf16[192,8,512]{2,0,1:T(8,128)(2,1)}), bf16[192,8,512]{2,0,1:T(8,128)(2,1)}, u32[]{:S(2)}, u32[]{:S(2)}) %all-to-all-start.1) | async-done | bytes 1572896 | tf_op jit(solution)/shard_map/all_to_all | solution.py:93
  221.0 5.5 %multiply_bitcast_fusion.1 = f32[1,1024,512]{2,1,0:T(8,128)} fusion(bf16[1536,512]{1,0:T(8,128)(2,1)} %bitcast.2, bf16[1536,2816]{1,0:T(8,128)(2,1)} %all-gather.3.cloned.1.call-done, f32[]{:T(128)S(6)} %div.27), kind=kOutput, calls=%fused_computation.6 | convolution fusion | flops 1611137024 | bytes 6815748 | tf_op jit(solution)/shard_map/dot_general | solution.py:34
  (5 shorter events, 0.1 us)
Async XLA Ops:
  7.2 4.9 %copy-start = (bf16[64,1024]{1,0:T(8,128)(2,1)S(1)}, bf16[64,1024]{1,0:T(8,128)(2,1)}, u32[]{:S(2)}) copy-start(bf16[64,1024]{1,0:T(8,128)(2,1)} %param.4) | copy-start | bytes 393220
  7.2 132.1 %all-gather.5.cloned.1.call-start = ((), (), s32[]{:S(2)}) async-start(), calls=%async_computation.6 | async-start | bytes 1966080 | tf_op jit(solution)/shard_map/all_gather | solution.py:87
  63.8 1.1 copy-start.1
  64.7 137.0 %all-gather.3.cloned.1.call-start = ((), (), s32[]{:S(2)}) async-start(), calls=%async_computation.5 | async-start | bytes 9732096 | tf_op jit(solution)/shard_map/all_gather | solution.py:30
  116.2 18.2 %all-to-all-start.2 = ((f32[64,1,8]{2,1,0:T(1,128)}), f32[64,1,8]{2,1,0:T(1,128)S(1)}, u32[]{:S(2)}, u32[]{:S(2)}) async-start(f32[64,1,8]{2,1,0:T(1,128)} %broadcast_in_dim.18), calls=%async_computation.2 | async-start | bytes 65536 | tf_op jit(solution)/shard_map/all_to_all | solution.py:16
  134.4 61.1 %all-to-all-start.4 = ((bf16[192,8,896]{2,0,1:T(8,128)(2,1)}), bf16[192,8,896]{2,0,1:T(8,128)(2,1)S(1)}, u32[]{:S(2)}, u32[]{:S(2)}) async-start(bf16[192,8,896]{2,0,1:T(8,128)(2,1)} %copy.53), calls=%async_computation.4 | async-start | bytes 5505024 | tf_op jit(solution)/shard_map/all_to_all | solution.py:94
  195.5 25.4 %all-to-all-start.1 = ((bf16[192,8,512]{2,0,1:T(8,128)(2,1)}), bf16[192,8,512]{2,0,1:T(8,128)(2,1)}, u32[]{:S(2)}, u32[]{:S(2)}) async-start(bf16[192,8,512]{2,0,1:T(8,128)(2,1)} %bitcast.20), calls=%async_computation.1 | async-start | bytes 3145728 | tf_op jit(solution)/shard_map/all_to_all | solution.py:93
Sparse Core Ops, SparseCore 0:
  64.8 51.0 all-gather.4
  117.7 72.3 all-gather.2
